TPU v7x, 32 devices: a whole 2x2x4 slice. The times are simulated.
32 devices in a mesh: seq: 8 (over z, x), head: 4 (over y, core).
Axes of the slice: x: 2, y: 2, z: 4, core: 2. Of those that a mesh axis runs over, the one named last changes fastest.
Arguments:
- inputs: bfloat16 [2048, 3072], P('seq'), may hold values from -6 to 6
- decay_logs: float32 [12, 2048], P('head', 'seq'), may hold values from -3 to 0
- query_retain: bfloat16 [3072, 1536], P('seq', 'head'), may hold values from -0.109375 to 0.109375
- key_retain: bfloat16 [3072, 1536], P('seq', 'head'), may hold values from -0.109375 to 0.109375
- value_retain: bfloat16 [3072, 1536], P('seq', 'head'), may hold values from -0.109375 to 0.109375
- output_retain: bfloat16 [3072, 1536], P('seq', 'head'), may hold values from -0.15625 to 0.15625
- key_global: bfloat16 [3072, 512], P('seq', 'head')
- value_global: bfloat16 [3072, 512], P('seq', 'head'), may hold values from -0.109375 to 0.109375
- query_cross: bfloat16 [3072, 1536], P('seq', 'head')
Outputs:
- decoded: float32 [2048, 3072], P('seq')
- attended: bfloat16 [2048, 1536], P('seq', 'head')
All inputs are finite; a program needn't handle non-finite values.
Results may differ from a plain program's by a relative error of at most 0.028.
Values may be sent and summed in bfloat16 or wider, within the bound.
A program may use at most 192 MiB of HBM per device.

v0:
```python
import functools

import jax
import jax.numpy as jnp
from jax import lax
from jax.experimental import pallas as pl
from jax.experimental.pallas import tpu as pltpu
from jax.sharding import PartitionSpec as P

HD = 128
F32 = jnp.float32
BF16 = jnp.bfloat16
MESH = pl.DeviceIdType.MESH
KEY, VALUE, QUERY, OUT, KEY_GLOBAL, VALUE_GLOBAL, CROSS = 0, 1, 2, 3, 6, 7, 8
OUTS, LAST, ALL = range(3, 6), range(6, 11), range(11)
PLUS = (True, False, True) + (False,) * 3 + (True, False, True, False, True)


def dot(a, b, dims=((1,), (0,)), precision=None):
    return lax.dot_general(a, b, (dims, ((), ())), precision=precision, preferred_element_type=F32)


def kernel(
    n, aligned,
    x_ref, xs_ref, decay_ref,
    wk_ref, wv_ref, wq_ref, wo_ref, wc_ref, wkg_ref, wvg_ref,
    mix_ref, att_ref,
    gk, gv, gq, go, gc, gkg, gvg, tots, states, kvs,
    run_row_ref, run_col_ref, tot_ref, dec_ref, nx, twin_nx, sent, got, within_buf,
    normed, q_buf, k_buf, v_buf, ret, part, got_a, pair, got_b, mine, got_c,
    q_rows, top, total, acc,
    wp_send, wm_send, w_recv, wx_send, w_local, t_send, t_recv,
    s_send, s_recv, sx_send, kv_send, kv_recv, kvx_send, h_send, h_recv, p_send, p_recv,
):
    me = lax.axis_index("seq")
    head = lax.axis_index("head")
    rows, width = x_ref.shape
    heads = wq_ref.shape[1] // HD
    half_n = n // 2
    mid = half_n // 2
    odd = lax.rem(me, 2)
    twin = me + 1 - 2 * odd
    core = lax.rem(head, 2)
    near = head + 1 - 2 * core
    far = lax.rem(head + 2, 4)
    def columns(ref):
        return tuple(ref.at[:, h * HD:(h + 1) * HD] for h in range(heads))

    own_refs = (wk_ref, wv_ref, wq_ref, *columns(wo_ref), wkg_ref, wvg_ref, *columns(wc_ref))
    full_refs = (gk, gv, gq, *columns(go), gkg, gvg, *columns(gc))
    up = lax.rem(me + 2, n)
    down = lax.rem(me + n - 2, n)

    barrier = pltpu.get_barrier_semaphore()

    @pl.loop(0, n - 1)
    def _(k):
        pl.semaphore_signal(
            barrier, inc=1, device_id={"seq": lax.rem(me + 1 + k, n)}, device_id_type=MESH
        )

    for other in (near, far):
        pl.semaphore_signal(barrier, inc=1, device_id={"head": other}, device_id_type=MESH)
    pl.semaphore_wait(barrier, n + 1)

    def slot(m, o):
        depth = wq_ref.shape[0]
        place = o // 2 if m < OUT else o
        return full_refs[m].at[pl.ds(pl.multiple_of(place * depth, depth), depth), :]

    def ring_copy(m, s, plus):
        o = lax.rem(me + n - 2 * s, n) if plus else lax.rem(me + 2 * s, n)
        src = own_refs[m] if s == 0 else slot(m, o)
        return pltpu.make_async_remote_copy(
            src, slot(m, o), (wp_send if plus else wm_send).at[m, s], w_recv.at[m, o],
            device_id={"seq": up if plus else down}, device_id_type=MESH)

    def x_copy(m, o, own=False):
        return pltpu.make_async_remote_copy(
            own_refs[m] if own else slot(m, o), slot(m, o), wx_send.at[m, o // 2], w_recv.at[m, o],
            device_id={"seq": twin}, device_id_type=MESH)

    def local_copy(m):
        return pltpu.make_async_copy(own_refs[m], slot(m, me), w_local.at[m])

    def start_gather(m):
        ring_copy(m, 0, True).start()
        ring_copy(m, 0, False).start()
        local_copy(m).start()

    def arrive(m, o):
        x_copy(m, o).wait_recv()

    def forward(m):
        for s in range(1, mid):
            for plus in (True, False):
                o = lax.rem(me + n - 2 * s, n) if plus else lax.rem(me + 2 * s, n)
                arrive(m, o)
                if s < mid - 1 or plus == PLUS[m]:
                    ring_copy(m, s, plus).start()
                if m >= OUT:
                    x_copy(m, o).start()

    def settle(m):
        o = lax.rem(me + 2 * mid, n)
        arrive(m, o)
        if m >= OUT:
            x_copy(m, o).start()
        local_copy(m).wait()

    def finish(m):
        @pl.loop(0, half_n)
        def _(k):
            arrive(m, lax.rem(twin + 2 * k, n))

    def finish_sends(m):
        for s in range(mid):
            for plus in (True, False):
                if s < mid - 1 or plus == PLUS[m]:
                    ring_copy(m, s, plus).wait_send()
        if m >= OUT:
            x_copy(m, me, own=True).wait_send()

            @pl.loop(1, half_n)
            def _(k):
                x_copy(m, lax.rem(me + 2 * k, n)).wait_send()

    z = me // 2

    def causal_ops(buf, send, recv, x_send):
        def direct(k):
            return pltpu.make_async_remote_copy(
                buf.at[me], buf.at[me], send.at[k], recv.at[me],
                device_id={"seq": me + 2 * k}, device_id_type=MESH)

        def across(o, k):
            return pltpu.make_async_remote_copy(
                buf.at[o], buf.at[o], x_send.at[k], recv.at[o],
                device_id={"seq": twin}, device_id_type=MESH)

        def start():
            @pl.when(odd == 0)
            def _():
                across(me, 0).start()

            @pl.loop(1, half_n - z)
            def _(k):
                direct(k).start()

        def relay(use=None):
            @pl.loop(1, z + 1)
            def _(k):
                o = me - 2 * k
                across(o, k).wait_recv()
                across(o, k).start()
                if use is not None:
                    use(o)

        def finish(use=None):
            @pl.loop(0, z + odd)
            def _(k):
                across(me - 1 - 2 * k, 0).wait_recv()
                if use is not None:
                    use(me - 1 - 2 * k)

        def finish_sends():
            @pl.when(odd == 0)
            def _():
                across(me, 0).wait_send()

            @pl.loop(1, half_n - z)
            def _(k):
                direct(k).wait_send()

            @pl.loop(1, z + 1)
            def _(k):
                across(me - 2 * k, k).wait_send()

        return start, relay, finish, finish_sends

    def total_copy(p):
        return pltpu.make_async_remote_copy(
            tot_ref, tots.at[me], t_send.at[p], t_recv.at[me],
            device_id={"seq": p}, device_id_type=MESH)

    start_gather(KEY)
    start_gather(VALUE)
    depth = wq_ref.shape[0]
    t_iota = lax.broadcasted_iota(jnp.int32, (rows, rows), 0)
    s_iota = lax.broadcasted_iota(jnp.int32, (rows, rows), 1)
    run_row_ref[...] = jnp.zeros_like(run_row_ref)
    run_row_ref[:heads, :] = decay_ref[...]
    lower = (s_iota <= t_iota).astype(F32)
    logs = run_row_ref[...]
    run_col_ref[...] = dot(lower, logs, ((1,), (1,)), lax.Precision.HIGHEST)
    run_row_ref[...] = dot(logs, lower, ((1,), (1,)), lax.Precision.HIGHEST)
    tot_ref[...] = jnp.broadcast_to(run_row_ref[:, rows - 1:rows], tot_ref.shape)

    @pl.loop(0, rows // 32)
    def _(i):
        part_rows = pl.ds(i * 32, 32)
        x = x_ref[part_rows, :].astype(F32)
        scale = lax.rsqrt(jnp.mean(x * x, axis=-1, keepdims=True) + 1e-06)
        for side in range(2):
            if aligned:
                for j in range(half_n):
                    cols = slice((2 * j + side) * depth, (2 * j + side + 1) * depth)
                    nx[side, part_rows, j * depth:(j + 1) * depth] = (
                        x_ref[part_rows, cols].astype(F32) * scale).astype(BF16)
            else:
                nx[side, part_rows, :] = (
                    xs_ref[side, part_rows, :].astype(F32) * scale).astype(BF16)

    def twin_copy(src, dst, i):
        return pltpu.make_async_remote_copy(
            src, dst, p_send.at[i], p_recv.at[i], device_id={"seq": twin}, device_id_type=MESH)

    tokens = twin_copy(nx.at[1 - odd], twin_nx, 3)
    tokens.start()
    for m in (*OUTS, *LAST):
        x_copy(m, me, own=True).start()

    @pl.loop(me + 1, n)
    def _(p):
        total_copy(p).start()

    def share(m):
        twin_part = dot(twin_nx[...], full_refs[m][...])
        sent[m] = twin_part.astype(BF16)
        twin_copy(sent.at[m], got.at[m], m).start()
        return dot(nx[odd], full_refs[m][...])

    def combine(m, own, dst):
        twin_copy(sent.at[m], got.at[m], m).wait_recv()
        dst[...] = (own + got[m].astype(F32)).astype(BF16)

    forward(KEY)
    forward(VALUE)
    start_gather(QUERY)
    tokens.wait_recv()
    settle(KEY)
    within_buf[...] = share(KEY)
    settle(VALUE)
    value_part = share(VALUE)
    combine(KEY, within_buf[...], k_buf)
    combine(VALUE, value_part, v_buf)
    forward(QUERY)
    for h in range(heads):
        cols = slice(h * HD, (h + 1) * HD)
        col = run_col_ref[:, h:h + 1]
        tail = jnp.exp(run_row_ref[h:h + 1, rows - 1:rows] - col)
        faded = (k_buf[:, cols].astype(F32) * tail).astype(BF16)
        states[me, cols, :] = dot(faded, v_buf[:, cols], ((0,), (0,))).astype(BF16)
    s_start, s_relay, s_finish, s_done = causal_ops(states, s_send, s_recv, sx_send)
    s_start()
    for m in OUTS:
        start_gather(m)
    settle(QUERY)
    query_part = share(QUERY)
    combine(QUERY, query_part, q_buf)
    for h in range(heads):
        cols = slice(h * HD, (h + 1) * HD)
        col = run_col_ref[:, h:h + 1]
        causal = t_iota >= s_iota
        spread = jnp.where(causal, col - run_row_ref[h:h + 1, :], 0.0)
        decay = jnp.where(causal, jnp.exp(spread), 0.0)
        scores = dot(q_buf[:, cols], k_buf[:, cols], ((1,), (1,)))
        weighted = (scores * decay).astype(BF16)
        within_buf[:, cols] = dot(weighted, v_buf[:, cols])

    for m in OUTS:
        forward(m)
    for m in LAST:
        start_gather(m)

    @pl.loop(0, me)
    def _(o):
        pltpu.make_async_remote_copy(
            tots.at[o], tots.at[o], t_send.at[o], t_recv.at[o],
            device_id={"seq": twin}, device_id_type=MESH).wait_recv()

    s_relay()
    s_finish()
    for h in range(heads):
        cols = slice(h * HD, (h + 1) * HD)
        col = run_col_ref[:, h:h + 1]

        def step(o, state):
            return jnp.exp(tots[o, h:h + 1, :]) * state + states[o, cols, :].astype(F32)

        incoming = lax.fori_loop(0, me, step, jnp.zeros((HD, HD), F32))
        carried = dot(
            q_buf[:, cols].astype(F32), incoming, precision=lax.Precision.HIGHEST) * jnp.exp(col)
        raw = within_buf[:, cols] + carried
        ret[:, cols] = (
            raw * lax.rsqrt(jnp.mean(raw * raw, axis=-1, keepdims=True) + 1e-06)).astype(BF16)

    half = width // 2
    piece = half // 3

    def head_copy(src, dst, i, other):
        return pltpu.make_async_remote_copy(
            src, dst, h_send.at[i], h_recv.at[i], device_id={"head": other}, device_id_type=MESH)

    def project(side):
        for c in range(3):
            base = pl.multiple_of(side * half + c * piece, piece)
            term = dot(ret[...], go[pl.ds(base, piece), :], ((1,), (1,)))
            part[side, :, c * piece:(c + 1) * piece] = term.astype(BF16)

    for m in OUTS:
        settle(m)
    for m in OUTS:
        finish(m)
    project(1 - core)
    to_near = head_copy(part.at[1 - core], got_a, 0, near)
    to_near.start()
    project(core)
    to_near.wait_recv()
    pair[...] = (part[core].astype(F32) + got_a[...].astype(F32)).astype(BF16)
    to_far = head_copy(pair, got_b, 1, far)
    to_far.start()
    for m in LAST:
        forward(m)
    to_far.wait_recv()
    mine[...] = (pair[...].astype(F32) + got_b[...].astype(F32)).astype(BF16)
    back = head_copy(mine, got_c, 2, near)
    back.start()
    for m in LAST:
        settle(m)
    own_cols = pl.ds(pl.multiple_of(core * half, half), half)
    mix_ref[:, own_cols] = mine[...]
    dec_ref[:, own_cols] = x_ref[:, own_cols].astype(F32) + mine[...].astype(F32)
    back.wait_recv()
    other_cols = pl.ds(pl.multiple_of((1 - core) * half, half), half)
    mix_ref[:, other_cols] = got_c[...]
    dec_ref[:, other_cols] = x_ref[:, other_cols].astype(F32) + got_c[...].astype(F32)

    @pl.loop(0, rows // 32)
    def _(i):
        part_rows = pl.ds(i * 32, 32)
        d = dec_ref[part_rows, :]
        normed[part_rows, :] = (
            d * lax.rsqrt(jnp.mean(d * d, axis=-1, keepdims=True) + 1e-06)).astype(BF16)

    finish(KEY_GLOBAL)
    finish(VALUE_GLOBAL)
    kvs[me, :, :HD] = dot(normed[...], gkg[...]).astype(BF16)
    kvs[me, :, HD:] = dot(normed[...], gvg[...]).astype(BF16)
    kv_start, kv_relay, kv_finish, kv_done = causal_ops(kvs, kv_send, kv_recv, kvx_send)
    kv_start()
    for m in LAST[2:]:
        finish(m)
    cross = (dot(normed[...], gc[...]) * HD ** -0.5).astype(BF16)
    for g in range(heads):
        q_rows[g * rows:(g + 1) * rows, :] = cross[:, g * HD:(g + 1) * HD]

    for g in range(heads):
        block = slice(g * rows, (g + 1) * rows)
        scores = dot(q_rows[block, :], kvs[me, :, :HD], ((1,), (1,)))
        scores = jnp.where(t_iota >= s_iota, scores, -1e30)
        high = jnp.max(scores, axis=-1, keepdims=True)
        weights = jnp.exp(scores - high)
        top[block, :] = high
        total[block, :] = jnp.sum(weights, axis=-1, keepdims=True)
        acc[block, :] = dot(weights.astype(BF16), kvs[me, :, HD:])

    def attend(o):
        for g in range(heads):
            block = slice(g * rows, (g + 1) * rows)
            scores = dot(q_rows[block, :], kvs[o, :, :HD], ((1,), (1,)))
            old = top[block, :]
            high = jnp.maximum(old, jnp.max(scores, axis=-1, keepdims=True))
            weights = jnp.exp(scores - high)
            shrink = jnp.exp(old - high)
            top[block, :] = high
            total[block, :] = total[block, :] * shrink + jnp.sum(weights, axis=-1, keepdims=True)
            acc[block, :] = acc[block, :] * shrink + dot(weights.astype(BF16), kvs[o, :, HD:])

    kv_relay(attend)
    kv_finish(attend)

    for g in range(heads):
        block = slice(g * rows, (g + 1) * rows)
        att_ref[:, g * HD:(g + 1) * HD] = (acc[block, :] / total[block, :]).astype(BF16)

    @pl.loop(me + 1, n)
    def _(p):
        total_copy(p).wait_send()

    for m in ALL:
        finish_sends(m)
    tokens.wait_send()
    for m in range(3):
        twin_copy(sent.at[m], got.at[m], m).wait_send()

    s_done()
    kv_done()
    to_near.wait_send()
    to_far.wait_send()
    back.wait_send()


def body(n, inputs, decay_logs, wq, wk, wv, wo, kg, vg, qc):
    rows, width = inputs.shape
    inner = wq.shape[1]
    heads = inner // HD
    depth = wq.shape[0]
    aligned = depth % HD == 0
    half_n = n // 2
    half = width // 2
    small = inputs[:16, :HD].reshape(1, 16, HD)
    split = inputs.reshape(rows, half_n, 2, depth).transpose(2, 0, 1, 3).reshape(2, rows, half)
    vmem = pl.BlockSpec(memory_space=pltpu.VMEM)
    dma = pltpu.SemaphoreType.DMA
    mid = max(half_n // 2, 1)
    mixed, attended = pl.pallas_call(
        functools.partial(kernel, n, aligned),
        out_shape=(
            jax.ShapeDtypeStruct((rows, width), BF16),
            jax.ShapeDtypeStruct((rows, inner), BF16),
        ),
        in_specs=[vmem] * 10,
        out_specs=(vmem, vmem),
        scratch_shapes=[
            pltpu.VMEM((half, inner), BF16),
            pltpu.VMEM((half, inner), BF16),
            pltpu.VMEM((half, inner), BF16),
            pltpu.VMEM((width, inner), BF16),
            pltpu.VMEM((width, inner), BF16),
            pltpu.VMEM((width, HD), BF16),
            pltpu.VMEM((width, HD), BF16),
            pltpu.VMEM((n, 8, HD), F32),
            pltpu.VMEM((n, inner, HD), BF16),
            pltpu.VMEM((n, rows, 2 * HD), BF16),
            pltpu.VMEM((8, rows), F32),
            pltpu.VMEM((rows, 8), F32),
            pltpu.VMEM((8, HD), F32),
            pltpu.VMEM((rows, width), F32),
            pltpu.VMEM((2, rows, half), BF16),
            pltpu.VMEM((rows, half), BF16),
            pltpu.VMEM((3, rows, inner), BF16),
            pltpu.VMEM((3, rows, inner), BF16),
            pltpu.VMEM((rows, inner), F32),
            pltpu.VMEM((rows, width), BF16),
            pltpu.VMEM((rows, inner), BF16),
            pltpu.VMEM((rows, inner), BF16),
            pltpu.VMEM((rows, inner), BF16),
            pltpu.VMEM((rows, inner), BF16),
            pltpu.VMEM((2, rows, half), BF16),
            pltpu.VMEM((rows, half), BF16),
            pltpu.VMEM((rows, half), BF16),
            pltpu.VMEM((rows, half), BF16),
            pltpu.VMEM((rows, half), BF16),
            pltpu.VMEM((rows, half), BF16),
            pltpu.VMEM((heads * rows, HD), BF16),
            pltpu.VMEM((heads * rows, 1), F32),
            pltpu.VMEM((heads * rows, 1), F32),
            pltpu.VMEM((heads * rows, HD), F32),
            dma((11, mid)), dma((11, mid)), dma((11, n)), dma((11, half_n)), dma((11,)),
            dma((n,)), dma((n,)),
            dma((half_n,)), dma((n,)), dma((half_n,)),
            dma((half_n,)), dma((n,)), dma((half_n,)),
            dma((3,)), dma((3,)), dma((4,)), dma((4,)),
        ],
        compiler_params=pltpu.CompilerParams(
            collective_id=0, has_side_effects=True, vmem_limit_bytes=62 * 1024 * 1024),
        name="layer",
    )(inputs, small if aligned else split, decay_logs, wk, wv, wq, wo, qc, kg, vg)
    return inputs.astype(F32) + mixed.astype(F32), attended


def solution(mesh):
    n = mesh.shape["seq"]

    def run(*args):
        return body(n, *args)

    in_specs = (P("seq", None), P("head", "seq")) + (P("seq", "head"),) * 7
    out_specs = (P("seq", None), P("seq", "head"))
    return jax.shard_map(run, mesh=mesh, in_specs=in_specs, out_specs=out_specs, check_vma=False)
```

profile of v0, /device:TPU:24, one launch (start us, length us, event | category | flops | bytes accessed | tf_op | source)
XLA Modules:
  0.0 165.1 jit_solution(3726353527427722215)
XLA Ops:
  0.6 1.3 slice_bitcast_fusion.xs_ref
  1.9 0.0 copy-start
  1.9 158.9 %layer.1 = (bf16[256,3072]{1,0:T(8,128)(2,1)}, bf16[256,384]{1,0:T(8,128)(2,1)}) custom-call(bf16[256,3072]{1,0:T(8,128)(2,1)} %x_ref.1, bf16[1,16,128]{2,1,0:T(8,128)(2,1)} %slice_bitcast_fusion.xs_ref, f32[3,256]{1,0:T(4,128)} %decay_ref.1, bf16[384,384]{1,0:T(8,128)(2,1)} %wk_ref.1, bf16[384,384]{1,0:T(8,128)(2,1)} %wv_ref.1, bf16[384,384]{1,0:T(8,128)(2,1)} %wq_ref.1, ...), custom_call_target="tpu_custom_call" | custom-call | tf_op jit(solution)/shard_map/layer/pallas_call | solution.py:417
  160.8 0.0 copy-done
  160.8 0.0 copy-start.1
  160.8 3.6 %convert_add_fusion = f32[256,3072]{1,0:T(8,128)} fusion(bf16[256,3072]{1,0:T(8,128)(2,1)} %get-tuple-element.4, bf16[256,3072]{1,0:T(8,128)(2,1)S(1)} %copy-done), kind=kLoop, calls=%fused_computation | loop fusion | flops 2359296 | bytes 6291456 | tf_op jit(solution)/shard_map/add | solution.py:470
  164.5 0.0 copy-done.1
  164.5 0.7 copy.12
Async XLA Ops:
  1.9 158.9 %copy-start = (bf16[256,3072]{1,0:T(8,128)(2,1)S(1)}, bf16[256,3072]{1,0:T(8,128)(2,1)}, u32[]{:S(2)}) copy-start(bf16[256,3072]{1,0:T(8,128)(2,1)} %x_ref.1) | copy-start | bytes 4718596
  160.8 3.6 %copy-start.1 = (bf16[256,384]{1,0:T(8,128)(2,1)S(1)}, bf16[256,384]{1,0:T(8,128)(2,1)}, u32[]{:S(2)}) copy-start(bf16[256,384]{1,0:T(8,128)(2,1)} %get-tuple-element.9) | copy-start | bytes 589828
where the time goes:
time: 167 us; the launch traced here: 165 us
  Pallas kernels  159 us (95%)
  other arithmetic  3.63 us (2%)
  local copies, waits for them, and re-layouts  1.97 us (1%)
    pallas_call x1, Pallas kernels, body(): pl.pallas_call(functools.partial(kernel, n, aligned), out_shape=(jax.Shap...  159 us
    add x1, other arithmetic, body(): return (inputs.astype(F32) + mixed.astype(F32), attended)  3.63 us

commit v1 on v0

v1 whole, which is shorter than its diff:
```python
import functools

import jax
import jax.numpy as jnp
from jax import lax
from jax.experimental import pallas as pl
from jax.experimental.pallas import tpu as pltpu
from jax.sharding import PartitionSpec as P

HD = 128
QUAD = 4
EXACT = 16
LATE = 4
LAG = 3
F32 = jnp.float32
BF16 = jnp.bfloat16
MESH = pl.DeviceIdType.MESH
SPOT = (0, 2, 1, 3)


def dot(a, b, dims=((1,), (0,)), precision=None):
    return lax.dot_general(a, b, (dims, ((), ())), precision=precision, preferred_element_type=F32)


def kernel(n, aligned, *refs):
    it = iter(refs)
    take = lambda k: tuple(next(it) for _ in range(k))
    decay_ref, x_in = take(2)
    (xs_ref,) = (None,) if aligned else take(1)
    w_in = take(7)
    mix_ref, att_ref = take(2)
    wk_ref, wv_ref, wq_ref, wo_ref, wc_ref, wkg_ref, wvg_ref = w_in
    (x_ref,) = take(1)
    gw, go, gkv, gc, xq, tots, states, kvs = take(8)
    run_row_ref, run_col_ref, tot_ref, scale_ref = take(4)
    keep, xs, xr, zs, zr = take(5)
    q_buf, k_buf, v_buf, within_buf, rt = take(5)
    part, got_a, pair, got_b, mix, outm, dn, sq, sq_got = take(9)
    q_rows, top, acc = take(3)
    att_buf, in_sem, out_sem, att_sem = take(4)
    nq, fold, sx, sx_got, xh, xh_got, zh, zh_got = take(8)
    sx_send, sx_recv, xh_send, xh_recv, zh_send, zh_recv = take(6)
    (
        w_send, w_recv, x_send, x_recv, x_local,
        r1_send, r1_recv, r2_send, r2_recv, t_send, t_recv,
        s_send, s_recv, sq_send, sr_send, kv_send, kv_recv, kvq_send, kvr_send,
        a_send, a_recv, h_send, h_recv, q_send, q_recv, o_send, o_recv,
    ) = take(27)

    me = lax.axis_index("seq")
    head = lax.axis_index("head")
    rows, width = x_ref.shape
    depth, inner = wq_ref.shape
    heads = inner // HD
    blocks = n // QUAD
    kd = blocks * depth
    half = kd // 2
    odd = lax.rem(me, 2)
    across = 2 - 4 * lax.rem(me // 2, 2)
    twin = me + 1 - 2 * odd
    partner = (me, twin, me + across, twin + across)
    member = tuple(lax.rem(p, QUAD) for p in partner)
    place = me // QUAD
    inner_place = lax.rem(me // 2, 2) != lax.rem(place, 2)
    core = lax.rem(head, 2)
    near = head + 1 - 2 * core
    far = lax.rem(head + 2, 4)

    def columns(ref):
        return tuple(ref.at[:, h * HD:(h + 1) * HD] for h in range(heads))

    wk, wv, wq = columns(wk_ref), columns(wv_ref), columns(wq_ref)
    own = []
    for h in range(heads):
        own += [wk[h], wv[h]]
    own += wq
    first_out = len(own)
    own += list(columns(wo_ref))
    first_glob = len(own)
    own += [wkg_ref, wvg_ref, *columns(wc_ref)]
    count = len(own)

    def span(i):
        return slice(i * rows, (i + 1) * rows)

    def to_seq(src, dst, send, recv, other):
        return pltpu.make_async_remote_copy(
            src, dst, send, recv, device_id={"seq": other}, device_id_type=MESH)

    def to_head(src, dst, send, recv, other):
        return pltpu.make_async_remote_copy(
            src, dst, send, recv, device_id={"head": other}, device_id_type=MESH)

    def slot(i, o):
        at = pl.ds(pl.multiple_of(o * depth, depth), depth)
        if first_out <= i < first_glob:
            h = i - first_out
            return go.at[at, h * HD:(h + 1) * HD]
        if i < first_out:
            return gw.at[i, at, :]
        g = i - first_glob
        if g < 2:
            return gkv.at[at, g * HD:(g + 1) * HD]
        return gc.at[at, (g - 2) * HD:(g - 1) * HD]

    x_load = pltpu.make_async_copy(x_in, x_ref, in_sem.at[0])
    x_load.start()
    def group(i):
        return 0 if i < first_out else 1 if i < first_glob else 2 if i < first_glob + 2 else 3

    for i in range(count):
        pltpu.make_async_copy(own[i], slot(i, place), in_sem.at[1 + group(i)]).start()

    def whole(ref, sem):
        pltpu.make_async_copy(ref, ref, sem).wait()

    def gone(ref, sem):
        to_seq(ref, ref, sem, x_recv.at[0, 0], twin).wait_send()

    def group_refs(size):
        return (gw.at[:, :size, :], go.at[:size, :], gkv.at[:size, :], gc.at[:size, :])

    barrier = pltpu.get_barrier_semaphore()

    @pl.loop(0, n - 1)
    def _(k):
        pl.semaphore_signal(
            barrier, inc=1, device_id={"seq": lax.rem(me + 1 + k, n)}, device_id_type=MESH
        )

    for other in (near, far):
        pl.semaphore_signal(barrier, inc=1, device_id={"head": other}, device_id_type=MESH)
    pl.semaphore_wait(barrier, n + 1)

    upper = head // 2
    piece = rows // 2

    def x_view(k, ups, side):
        if aligned:
            at = pl.multiple_of((QUAD * side + member[k]) * depth, depth)
            return x_ref.at[ups, pl.ds(at, depth)]
        return xs_ref.at[member[k], ups, pl.ds(pl.multiple_of(side * half, half), half)]

    def some_rows(base, up):
        return pl.ds(pl.multiple_of(base + up * piece, piece), piece)

    def side_cols(side):
        return pl.ds(pl.multiple_of(side * half, half), half)

    def spread(src, dst, send, recv):
        def hop(k):
            return to_seq(src(k), dst(k, upper, core), send.at[0], recv.at[0, k - 1], partner[k])

        def to_far(k):
            ref = dst(k, upper, core)
            return to_head(ref, ref, send.at[0], recv.at[1, k - 1], far)

        def to_near(k):
            ref = dst(k, upper, core)
            return to_head(ref, ref, send.at[0], recv.at[2, k - 1], near)

        def to_near_too(k):
            ref = dst(k, 1 - upper, core)
            return to_head(ref, ref, send.at[0], recv.at[3, k - 1], near)

        def landed(order):
            for k in order:
                hop(k).wait_recv()
                to_far(k).start()
                to_near(k).start()

        def crossed(order):
            for k in order:
                to_far(k).wait_recv()
                to_near_too(k).start()

        def settled(k):
            to_near(k).wait_recv()
            to_near_too(k).wait_recv()

        def sent():
            gone(mix.at[:3], send.at[0])

        return hop, landed, crossed, settled, sent

    x_hop, x_landed, x_crossed, x_settled, x_sent = spread(
        lambda k: x_view(k, some_rows(0, upper), core),
        lambda k, up, side: xq.at[some_rows(SPOT[k] * rows, up), side_cols(side)],
        x_send, x_recv)

    def x_own(side):
        return pltpu.make_async_copy(
            x_view(0, slice(None), side), xq.at[span(0), side * half:(side + 1) * half], x_local.at[0])

    def w_copy(i, k):
        ref = slot(i, place)
        return to_seq(ref, ref, w_send.at[group(i)], w_recv.at[i, k - 1], lax.rem(me + QUAD * k, n))

    def w_from(i, k):
        ref = slot(i, lax.rem(place + blocks - k, blocks))
        return to_seq(ref, ref, w_send.at[group(i)], w_recv.at[i, k - 1], twin)

    def w_start(i):
        @pl.loop(1, blocks)
        def _(k):
            w_copy(i, k).start()

    def w_wait(i):
        @pl.loop(1, blocks)
        def _(k):
            w_from(i, k).wait_recv()

    x_load.wait()
    for k in (2, 3, 1):
        x_hop(k).start()
    for i, ref in enumerate(group_refs(depth)):
        whole(ref, in_sem.at[1 + i])

    def starts(here, which):
        @pl.when(here)
        def _():
            for i in which:
                w_start(i)

    outer_place = jnp.logical_not(inner_place)
    starts(inner_place, range(first_out))
    starts(outer_place, range(LATE))
    for side in range(2):
        x_own(side).start()

    @pl.loop(0, n)
    def _(o):
        kvs[o, :, 2 * HD:] = jnp.ones((rows, HD), BF16)

    t_iota = lax.broadcasted_iota(jnp.int32, (rows, rows), 0)
    s_iota = lax.broadcasted_iota(jnp.int32, (rows, rows), 1)
    run_row_ref[...] = jnp.zeros_like(run_row_ref)
    run_row_ref[:heads, :] = decay_ref[...]
    lower = (s_iota <= t_iota).astype(F32)
    logs = run_row_ref[...]
    run_col_ref[...] = dot(lower, logs, ((1,), (1,)), lax.Precision.HIGHEST)
    run_row_ref[...] = dot(logs, lower, ((1,), (1,)), lax.Precision.HIGHEST)
    tot_ref[...] = jnp.broadcast_to(run_row_ref[:, rows - 1:rows], tot_ref.shape)

    def total_copy(p):
        return to_seq(tot_ref, tots.at[me], t_send.at[p], t_recv.at[me], p)

    @pl.loop(me + 1, n)
    def _(p):
        total_copy(p).start()

    @pl.loop(0, rows // 32)
    def _(i):
        part_rows = pl.ds(i * 32, 32)
        sums_ = jnp.zeros((32, HD), F32)
        for c in range(width // HD):
            x = x_ref[part_rows, c * HD:(c + 1) * HD].astype(F32)
            sums_ = sums_ + x * x
        fold[part_rows, :] = sums_

    ones = jnp.ones((8, HD), F32)
    eye = (s_iota == t_iota).astype(F32)
    sx[...] = dot(ones, fold[...], ((1,), (1,)), lax.Precision.HIGHEST)

    def row_copy(k):
        return to_seq(sx, sx_got.at[k], sx_send.at[0], sx_recv.at[k - 1], partner[k])

    for k in (1, 2, 3):
        row_copy(k).start()

    def scale_of(row):
        column = dot(eye, row, ((1,), (1,)), lax.Precision.HIGHEST)
        return lax.rsqrt(column[:, :1] / width + 1e-06)

    def normalise(k):
        scale_ref[...] = scale_of(sx[...] if k == 0 else sx_got[k])
        start = SPOT[k] * rows

        @pl.loop(0, rows // 32)
        def _(i):
            at = pl.ds(pl.multiple_of(start + i * 32, 32), 32)
            nq[at, :] = (
                xq[at, :].astype(F32) * scale_ref[pl.ds(pl.multiple_of(i * 32, 32), 32), :]
            ).astype(BF16)

    def hop_one(j, part_, first):
        return to_seq(xs.at[j, part_], xr.at[j, part_], r1_send.at[0],
                      r1_recv.at[j, part_], partner[first])

    def hop_two(j, first):
        return to_seq(zs.at[j], zr.at[j], r2_send.at[0], r2_recv.at[j], partner[3 - first])

    def exact_one(j):
        return to_seq(xh.at[j], xh_got.at[j], xh_send.at[0], xh_recv.at[j], partner[1])

    def exact_two(j):
        return to_seq(zh.at[j], zh_got.at[j], zh_send.at[0], zh_recv.at[j], partner[2])

    def rs_put(j, first, k, value):
        if k == first or k == 3:
            xs[j, k // 3] = value.astype(BF16)
            if j < first_out:
                xh[j, k // 3] = value[:EXACT]
        else:
            keep[j, (k + 1) // 2] = value

    def rs_send(j, first, k):
        if k == first or k == 3:
            hop_one(j, k // 3, first).start()

    def rs_begin(j, src):
        weights = gw[j]
        for k in (3, 1):
            rs_put(j, 1, k, dot(src[span(SPOT[k]), :], weights))
        exact_one(j).start()
        for k in (3, 1):
            rs_send(j, 1, k)
        for k in (2, 0):
            rs_put(j, 1, k, dot(src[span(SPOT[k]), :], weights))

    def rs_mid(j, first):
        hop_one(j, 1, first).wait_recv()
        zs[j] = (keep[j, 1] + xr[j, 1].astype(F32)).astype(BF16)
        hop_two(j, first).start()
        if j < first_out:
            exact_one(j).wait_recv()
            zh[j] = keep[j, 1, :EXACT] + xh_got[j, 1]
            exact_two(j).start()

    def rs_end(j, first):
        hop_one(j, 0, first).wait_recv()
        hop_two(j, first).wait_recv()
        value = keep[j, 0] + xr[j, 0].astype(F32) + zr[j].astype(F32)
        if j < first_out:
            exact_two(j).wait_recv()
            exact = keep[j, 0, :EXACT] + xh_got[j, 0] + zh_got[j]
            value = jnp.concatenate([exact, value[EXACT:]], axis=0)
        return value

    top_pair = lax.rem(me // 2, 2) == 1

    def causal_ops(view, send, recv, quad_send, relay_send):
        def later(k):
            return to_seq(view(me), view(me), send(k), recv(me), me + QUAD * k)

        def near_by(k):
            return to_seq(view(me), view(me), quad_send(k), recv(me), partner[k])

        def pass_on(k, j):
            o = me - QUAD * j
            return to_seq(view(o), view(o), relay_send(k, j), recv(o), partner[k])

        def second(j):
            o = partner[2] - QUAD * j
            sem = quad_send(3) if isinstance(j, int) else relay_send(3, j)
            return to_seq(view(o), view(o), sem, recv(o), twin)

        def land(o):
            to_seq(view(o), view(o), quad_send(1), recv(o), twin).wait_recv()

        def earlier(body):
            pl.loop(1, place + 1)(body)

        def start_far():
            @pl.loop(1, blocks - place)
            def _(k):
                later(k).start()

        def start():
            for k in (2, 1):
                @pl.when(partner[k] > me)
                def _():
                    near_by(k).start()

        def relay():
            @earlier
            def _(j):
                land(me - QUAD * j)
                for k in (2, 1):
                    pass_on(k, j).start()

        def relay_two():
            @pl.when(top_pair)
            def _():
                land(partner[2])
                second(0).start()

            @earlier
            def _(j):
                land(partner[2] - QUAD * j)
                second(j).start()

        def finish(use=lambda o: None):
            @earlier
            def _(j):
                use(me - QUAD * j)
                use(partner[2] - QUAD * j)

            @pl.when(top_pair)
            def _():
                use(partner[2])

            @pl.when(odd == 1)
            def _():
                land(twin)
                use(twin)

            @earlier
            def _(j):
                land(twin - QUAD * j)
                use(twin - QUAD * j)

        def finish_far(use=lambda o: None):
            @pl.when(top_pair)
            def _():
                land(partner[3])
                use(partner[3])

            @earlier
            def _(j):
                land(partner[3] - QUAD * j)
                use(partner[3] - QUAD * j)

        def finish_sends():
            @pl.loop(1, blocks - place)
            def _(k):
                later(k).wait_send()

            for k in (2, 1):
                @pl.when(partner[k] > me)
                def _():
                    near_by(k).wait_send()

            @pl.when(top_pair)
            def _():
                second(0).wait_send()

            @earlier
            def _(j):
                for k in (2, 1):
                    pass_on(k, j).wait_send()
                second(j).wait_send()

        return start_far, start, relay, relay_two, finish, finish_far, finish_sends

    state_ops = [
        causal_ops(
            lambda o, h=h: states.at[o, h * HD:(h + 1) * HD, :],
            lambda k, h=h: s_send.at[h, k - 1],
            lambda o, h=h: s_recv.at[h, o],
            lambda k, h=h: sq_send.at[h, k - 1],
            lambda k, j, h=h: sr_send.at[h, k - 1, j - 1],
        )
        for h in range(heads)
    ]

    def ret_copy(h, k):
        cols = slice(h * HD, (h + 1) * HD)
        return to_seq(rt.at[span(0), cols], rt.at[span(SPOT[k]), cols],
                      a_send.at[0], a_recv.at[h, k - 1], partner[k])

    def ret_relay(h):
        cols = slice(h * HD, (h + 1) * HD)
        return to_seq(rt.at[span(SPOT[2]), cols], rt.at[span(SPOT[3]), cols],
                      a_send.at[0], a_recv.at[h, 2], twin)

    def send_state(h):
        cols = slice(h * HD, (h + 1) * HD)
        tail = jnp.exp(run_row_ref[h:h + 1, rows - 1:rows] - run_col_ref[:, h:h + 1])
        faded = (k_buf[:, cols].astype(F32) * tail).astype(BF16)
        states[me, cols, :] = dot(faded, v_buf[:, cols], ((0,), (0,))).astype(BF16)
        state_ops[h][0]()
        state_ops[h][1]()

    def within(h):
        cols = slice(h * HD, (h + 1) * HD)
        causal = t_iota >= s_iota
        spread = jnp.where(causal, run_col_ref[:, h:h + 1] - run_row_ref[h:h + 1, :], 0.0)
        decay = jnp.where(causal, jnp.exp(spread), 0.0)
        scores = dot(q_buf[:, cols], k_buf[:, cols], ((1,), (1,)))
        weighted = (scores * decay).astype(BF16)
        within_buf[:, cols] = dot(weighted, v_buf[:, cols])

    def retain(h):
        cols = slice(h * HD, (h + 1) * HD)
        state_ops[h][4]()
        state_ops[h][5]()

        def step(o, state):
            return jnp.exp(tots[o, h:h + 1, :]) * state + states[o, cols, :].astype(F32)

        incoming = lax.fori_loop(0, me, step, jnp.zeros((HD, HD), F32))
        carried = dot(
            q_buf[:, cols].astype(F32), incoming, precision=lax.Precision.HIGHEST
        ) * jnp.exp(run_col_ref[:, h:h + 1])
        raw = within_buf[:, cols] + carried
        rt[span(0), cols] = (
            raw * lax.rsqrt(jnp.mean(raw * raw, axis=-1, keepdims=True) + 1e-06)).astype(BF16)
        ret_copy(h, 2).start()
        ret_copy(h, 1).start()

    x_landed((1, 2, 3))
    x_crossed((1, 2, 3))
    whole(xq.at[span(0), :], x_local.at[0])
    normalise(0)
    for k in (1, 2, 3):
        x_settled(k)
        row_copy(k).wait_recv()
        normalise(k)

    for i in range(first_out + LAG):
        if i < first_out:
            w_wait(i)
            if i + LATE < first_out:
                starts(outer_place, (i + LATE,))
            rs_begin(i, nq)
        if 1 <= i <= first_out:
            rs_mid(i - 1, 1)
        if i == first_out:
            for m in range(first_out, first_glob):
                w_start(m)
            for h in range(heads):
                state_ops[h][2]()
        if i == first_out + 1:
            for h in range(heads):
                state_ops[h][3]()
        if i < LAG:
            continue
        j = i - LAG
        value = rs_end(j, 1).astype(BF16)
        h, m = (j - 2 * heads, 2) if j >= 2 * heads else divmod(j, 2)
        (k_buf, v_buf, q_buf)[m][:, h * HD:(h + 1) * HD] = value
        if m == 1:
            send_state(h)
        if m == 2:
            within(h)

    @pl.loop(0, me)
    def _(o):
        to_seq(tots.at[o], tots.at[o], t_send.at[o], t_recv.at[o], twin).wait_recv()

    for h in range(heads):
        retain(h)
    w_start(first_glob)
    w_start(first_glob + 1)

    def near_copy(s):
        return to_head(part.at[s, 1 - core], got_a.at[s], h_send.at[0], h_recv.at[0, s], near)

    def far_copy(s):
        return to_head(pair.at[s], got_b.at[s], h_send.at[1], h_recv.at[1, s], far)

    def back_copy(s):
        ref = mix.at[s, core]
        return to_head(ref, ref, h_send.at[2], h_recv.at[2, s], near)

    for i in range(first_out, first_glob):
        w_wait(i)

    def project(s, side):
        part[s, side] = dot(
            rt[span(s), :], go[pl.ds(pl.multiple_of(side * half, half), half), :], ((1,), (1,))
        ).astype(BF16)

    def combine(s):
        near_copy(s).wait_recv()
        pair[s] = (part[s, core].astype(F32) + got_a[s].astype(F32)).astype(BF16)
        far_copy(s).start()

    trip = (SPOT[0], SPOT[1], SPOT[3], SPOT[2])
    for s in trip:
        if s == SPOT[1]:
            for h in range(heads):
                ret_copy(h, 2).wait_recv()
                ret_relay(h).start()
            for h in range(heads):
                ret_copy(h, 1).wait_recv()
        if s == SPOT[3]:
            for i in range(first_glob + 2, count):
                w_start(i)
            for h in range(heads):
                ret_relay(h).wait_recv()
        project(s, 1 - core)
        near_copy(s).start()
        project(s, core)
        combine(s)

    def square_copy(k):
        return to_seq(sq.at[SPOT[k]], sq_got.at[k], q_send.at[0], q_recv.at[k - 1], partner[k])

    out_hop, out_landed, out_crossed, out_settled, out_sent = spread(
        lambda k: mix.at[SPOT[k], core, some_rows(0, upper), :],
        lambda k, up, side: outm.at[k, side, some_rows(0, up), :],
        o_send, o_recv)

    kv_ops = causal_ops(
        lambda o: kvs.at[o, :, :2 * HD], lambda k: kv_send.at[k - 1], lambda o: kv_recv.at[o],
        lambda k: kvq_send.at[k - 1], lambda k, j: kvr_send.at[k - 1, j - 1])

    base = first_out
    def kv_part(k):
        value = dot(dn[span(SPOT[k]), :], gkv[...])
        for g in range(2):
            rs_put(base + g, 1, k, value[:, g * HD:(g + 1) * HD])
        for g in range(2):
            rs_send(base + g, 1, k)

    def kv_end(g):
        return (rs_end(base + g, 1) * scale_ref[...]).astype(BF16)

    turn = [1, 1] + [1 + g % 2 for g in range(heads)]

    def cross_part(k):
        value = dot(dn[span(SPOT[k]), :], gc[...])
        for g in crosses:
            rs_put(base + g, turn[g], k, value[:, (g - 2) * HD:(g - 1) * HD])
        for g in crosses:
            rs_send(base + g, turn[g], k)

    def cross_end(g):
        return rs_end(base + g, turn[g]) * scale_ref[...]

    crosses = tuple(range(2, 2 + heads))
    w_wait(first_glob)
    w_wait(first_glob + 1)
    for t, s in enumerate(trip):
        k = SPOT.index(s)
        far_copy(s).wait_recv()
        mix[s, core] = (pair[s].astype(F32) + got_b[s].astype(F32)).astype(BF16)
        back_copy(s).start()
        back_copy(s).wait_recv()
        squares = jnp.zeros((rows, HD), F32)
        for side in range(2):
            cols = slice(side * half, (side + 1) * half)
            d = xq[span(s), cols].astype(F32) + mix[s, side].astype(F32)
            dn[span(s), cols] = d.astype(BF16)
            for c in range(half // HD):
                lanes = d[:, c * HD:(c + 1) * HD]
                squares = squares + lanes * lanes
        kv_part(k)
        sq[s] = dot(ones, squares, ((1,), (1,)), lax.Precision.HIGHEST)
        if k:
            square_copy(k).start()
        if t == 2:
            out_hop(1).start()
            out_hop(3).start()
    rs_mid(base, 1)
    rs_mid(base + 1, 1)
    out_hop(2).start()
    for g in crosses:
        w_wait(first_glob + g)
    for k in (3, 1, 2, 0):
        cross_part(k)
    for k in (1, 2, 3):
        square_copy(k).wait_recv()
    squares = sq[0] + sq_got[1] + sq_got[2] + sq_got[3]
    scale_ref[...] = scale_of(squares)
    kvs[me, :, :HD] = kv_end(0)
    kvs[me, :, HD:2 * HD] = kv_end(1)
    kv_ops[0]()
    for g in crosses:
        rs_mid(base + g, turn[g])
    kv_ops[1]()
    out_landed((1, 3, 2))
    kv_ops[2]()
    for g in range(heads):
        block = span(g)
        q_rows[block, :] = (cross_end(2 + g) * HD ** -0.5).astype(BF16)
        scores = dot(q_rows[block, :], kvs[me, :, :HD], ((1,), (1,)))
        scores = jnp.where(t_iota >= s_iota, scores, -1e30)
        high = jnp.max(scores, axis=-1, keepdims=True)
        weights = jnp.exp(scores - high)
        top[block, :] = jnp.broadcast_to(high, (rows, HD))
        acc[block, :] = dot(weights.astype(BF16), kvs[me, :, HD:])
    kv_ops[3]()

    def attend(o):
        for g in range(heads):
            block = span(g)
            scores = dot(q_rows[block, :], kvs[o, :, :HD], ((1,), (1,)))
            old = top[block, :]
            high = jnp.maximum(old, jnp.max(scores, axis=-1, keepdims=True))
            weights = jnp.concatenate(
                [jnp.exp(scores[:, c:c + HD] - high) for c in range(0, rows, HD)], axis=1)
            shrink = jnp.exp(old - high)
            top[block, :] = high
            fresh = dot(weights.astype(BF16), kvs[o, :, HD:])
            for c in range(0, 2 * HD, HD):
                acc[block, c:c + HD] = acc[block, c:c + HD] * shrink + fresh[:, c:c + HD]

    def put(k, side):
        if aligned:
            at = pl.multiple_of((QUAD * side + member[k]) * depth, depth)
            dst = mix_ref.at[:, pl.ds(at, depth)]
        else:
            dst = mix_ref.at[member[k], :, side * half:(side + 1) * half]
        src = mix.at[0, side] if k == 0 else outm.at[k, side]
        return pltpu.make_async_copy(src, dst, out_sem.at[0])

    for side in range(2):
        put(0, side).start()
    kv_ops[4](attend)
    out_crossed((1, 3, 2))
    kv_ops[5](attend)
    for k in (2, 1, 3):
        out_settled(k)
        for side in range(2):
            put(k, side).start()

    def att_copy(g):
        cols = slice(g * HD, (g + 1) * HD)
        return pltpu.make_async_copy(att_buf.at[:, cols], att_ref.at[:, cols], att_sem.at[0])

    for g in range(heads):
        block = span(g)
        att_buf[:, g * HD:(g + 1) * HD] = (acc[block, :HD] / acc[block, HD:]).astype(BF16)
        att_copy(g).start()

    @pl.loop(me + 1, n)
    def _(p):
        total_copy(p).wait_send()

    for i, ref in enumerate(group_refs(kd - depth)):
        gone(ref, w_send.at[i])
    x_sent()
    out_sent()
    gone(xs, r1_send.at[0])
    gone(zs, r2_send.at[0])
    gone(sx_got.at[1:], sx_send.at[0])
    gone(xh, xh_send.at[0])
    gone(zh, zh_send.at[0])
    gone(sq.at[1:], q_send.at[0])
    gone(rt.at[rows:, :], a_send.at[0])
    for i in range(3):
        gone(pair, h_send.at[i])
    for h in range(heads):
        state_ops[h][6]()
    kv_ops[6]()
    whole(mix_ref, out_sem.at[0])
    whole(att_ref, att_sem.at[0])


def body(n, inputs, decay_logs, wq, wk, wv, wo, kg, vg, qc):
    rows, width = inputs.shape
    depth, inner = wq.shape
    heads = inner // HD
    blocks = n // QUAD
    kd = blocks * depth
    half = kd // 2
    aligned = depth % HD == 0 and blocks == 2
    vmem = pl.BlockSpec(memory_space=pltpu.VMEM)
    dma = pltpu.SemaphoreType.DMA
    sums = 4 * heads + 2
    count = 5 * heads + 2

    def bf(*shape):
        return pltpu.VMEM(shape, BF16)

    def f32(*shape):
        return pltpu.VMEM(shape, F32)

    args = [decay_logs, inputs]
    if not aligned:
        args.append(
            inputs.reshape(rows, blocks, QUAD, depth).transpose(2, 0, 1, 3).reshape(QUAD, rows, kd))
    args += [wk, wv, wq, wo, qc, kg, vg]
    anywhere = pl.BlockSpec(memory_space=pl.ANY)
    specs = [vmem, anywhere] + [vmem] * (not aligned) + [anywhere] * 7
    mixed_shape = (rows, width) if aligned else (QUAD, rows, kd)
    mixed, attended = pl.pallas_call(
        functools.partial(kernel, n, aligned),
        out_shape=(
            jax.ShapeDtypeStruct(mixed_shape, BF16),
            jax.ShapeDtypeStruct((rows, inner), BF16),
        ),
        in_specs=specs,
        out_specs=(anywhere, anywhere),
        scratch_shapes=[
            bf(rows, width),
            bf(3 * heads, kd, HD), bf(kd, inner), bf(kd, 2 * HD), bf(kd, inner), bf(QUAD * rows, kd),
            f32(n, 8, HD), bf(n, inner, HD), bf(n, rows, 3 * HD),
            f32(8, rows), f32(rows, 8), f32(8, HD), f32(rows, 1),
            f32(sums, 2, rows, HD), bf(sums, 2, rows, HD), bf(sums, 2, rows, HD),
            bf(sums, rows, HD), bf(sums, rows, HD),
            bf(rows, inner), bf(rows, inner), bf(rows, inner), f32(rows, inner),
            bf(QUAD * rows, inner),
            bf(QUAD, 2, rows, half), bf(QUAD, rows, half), bf(QUAD, rows, half),
            bf(QUAD, rows, half), bf(QUAD, 2, rows, half), bf(QUAD, 2, rows, half),
            bf(QUAD * rows, kd), f32(QUAD, 8, rows), f32(QUAD, 8, rows),
            bf(heads * rows, HD), f32(heads * rows, HD),
            f32(heads * rows, 2 * HD),
            bf(rows, inner), dma((5,)), dma((1,)), dma((1,)),
            bf(QUAD * rows, kd), f32(rows, HD), f32(8, rows), f32(QUAD, 8, rows),
            f32(3 * heads, 2, EXACT, HD), f32(3 * heads, 2, EXACT, HD),
            f32(3 * heads, EXACT, HD), f32(3 * heads, EXACT, HD),
            dma((1,)), dma((3,)), dma((1,)), dma((3 * heads,)), dma((1,)), dma((3 * heads,)),
            dma((4,)), dma((count, blocks - 1)),
            dma((1,)), dma((4, 3)), dma((1,)),
            dma((1,)), dma((sums, 2)), dma((1,)), dma((sums,)), dma((n,)), dma((n,)),
            dma((heads, blocks - 1)), dma((heads, n)), dma((heads, 3)), dma((heads, 3, blocks - 1)),
            dma((blocks - 1,)), dma((n,)), dma((3,)), dma((3, blocks - 1)),
            dma((1,)), dma((heads, 3)), dma((3,)), dma((3, QUAD)),
            dma((1,)), dma((3,)), dma((1,)), dma((4, 3)),
        ],
        compiler_params=pltpu.CompilerParams(
            collective_id=0, has_side_effects=True, vmem_limit_bytes=62 * 1024 * 1024),
        name="layer",
    )(*args)
    if not aligned:
        mixed = mixed.reshape(QUAD, rows, blocks, depth).transpose(1, 2, 0, 3).reshape(rows, width)
    return finish_rows(inputs, mixed, attended)


def finish_kernel(x_ref, mix_ref, att_in, dec_ref, att_ref):
    dec_ref[...] = x_ref[...].astype(F32) + mix_ref[...].astype(F32)
    att_ref[...] = att_in[...]


def finish_rows(inputs, mixed, attended):
    rows, width = inputs.shape
    inner = attended.shape[1]
    steps = 4
    wide = pl.BlockSpec((rows // steps, width), lambda i: (i, 0))
    thin = pl.BlockSpec((rows // steps, inner), lambda i: (i, 0))
    return pl.pallas_call(
        finish_kernel,
        grid=(steps,),
        out_shape=(
            jax.ShapeDtypeStruct((rows, width), F32),
            jax.ShapeDtypeStruct((rows, inner), BF16),
        ),
        in_specs=[wide, wide, thin],
        out_specs=(wide, thin),
        name="finish",
    )(inputs, mixed, attended)


def solution(mesh):
    n = mesh.shape["seq"]

    def run(*args):
        return body(n, *args)

    in_specs = (P("seq", None), P("head", "seq")) + (P("seq", "head"),) * 7
    out_specs = (P("seq", None), P("seq", "head"))
    return jax.shard_map(run, mesh=mesh, in_specs=in_specs, out_specs=out_specs, check_vma=False)
```

time: 167 us -> 129 us (0.77)
  Pallas kernels: 159 us -> 128 us
  other arithmetic: 3.63 us -> 0 us
  local copies, waits for them, and re-layouts: 1.97 us -> 0 us
    pallas_call x1, Pallas kernels: 159 us -> 124 us  [body(): pl.pallas_call(functools.partial(kernel, n, aligned), out_shape=(jax.Shap...]
    pallas_call x0 -> x1, Pallas kernels: none -> 4.23 us  [finish_rows(): pl.pallas_call(finish_kernel, grid=(steps,), out_shape=(jax.ShapeDtypeStr...]
    add x1 -> x0, other arithmetic: 3.63 us -> none  [body(): return (inputs.astype(F32) + mixed.astype(F32), attended)]
where the time goes in v1:
time: 129 us
  Pallas kernels  128 us (99%)
    pallas_call x1, Pallas kernels, body(): pl.pallas_call(functools.partial(kernel, n, aligned), out_shape=(jax.Shap...  124 us
    pallas_call x1, Pallas kernels, finish_rows(): pl.pallas_call(finish_kernel, grid=(steps,), out_shape=(jax.ShapeDtypeStr...  4.23 us

profile of v1, /device:TPU:24, one launch (start us, length us, event | category | flops | bytes accessed | tf_op | source)
XLA Modules:
  0.0 128.7 jit_solution(16133333966118358290)
XLA Ops:
  0.6 123.8 %layer.1 = (bf16[256,3072]{1,0:T(8,128)(2,1)}, bf16[256,384]{1,0:T(8,128)(2,1)}) custom-call(f32[3,256]{1,0:T(4,128)} %refs_0_.1, bf16[256,3072]{1,0:T(8,128)(2,1)} %x_ref.1, bf16[384,384]{1,0:T(8,128)(2,1)} %refs_2_.1, bf16[384,384]{1,0:T(8,128)(2,1)} %refs_3_.1, bf16[384,384]{1,0:T(8,128)(2,1)} %refs_4_.1, bf16[384,384]{1,0:T(8,128)(2,1)} %refs_5_.1, ...), custom_call_target="tpu_custom_call" | custom-call | tf_op jit(solution)/shard_map/layer/pallas_call | solution.py:770
  124.4 4.2 %finish.1 = (f32[256,3072]{1,0:T(8,128)}, bf16[256,384]{1,0:T(8,128)(2,1)}) custom-call(bf16[256,3072]{1,0:T(8,128)(2,1)} %x_ref.1, bf16[256,3072]{1,0:T(8,128)(2,1)} %get-tuple-element.4.mix_ref, bf16[256,384]{1,0:T(8,128)(2,1)} %get-tuple-element.5.att_in), custom_call_target="tpu_custom_call" | custom-call | tf_op jit(solution)/shard_map/finish/pallas_call | solution.py:825
